TPU v7x, 32 devices: a whole 2x2x4 slice. The times are simulated.
32 devices in a mesh: gx: 2 (over y), gy: 4 (over z), gz: 4 (over x, core).
Axes of the slice: x: 2, y: 2, z: 4, core: 2. Of those that a mesh axis runs over, the one named last changes fastest.
Arguments:
- eri: bfloat16 [1024, 256, 256], P(('gx', 'gy', 'gz')), may hold values from -0.375 to 0.375
- owner: int32 [1024, 1], P(('gx', 'gy', 'gz')), may hold values from 0 to 1; in each aligned block of 32 rows (0 to 31, 32 to 63, ...) at most 32 rows name the same one
- quartet: int32 [1024, 4], P(('gx', 'gy', 'gz')), may hold values from 0 to 191, as said below
- significance: int32 [1024], P(('gx', 'gy', 'gz')), may hold values 0 or 1
- density: bfloat16 [3072, 3072], P('gy'), may hold values from -6 to 6
Outputs:
- exchange: float32 [3072, 3072], P('gx', 'gy')
Inputs may be any that keep to these rules, and one draw needn't show every extreme that they name: Among the 32 tiles of one device (aligned blocks of 32 rows), no owner value is named more than 32 times, and in some blocks one is named exactly 32 times. `quartet`: column 0 lies in 0 to 23, column 1 in 0 to 191, column 2 in 0 to 47, column 3 in 0 to 191.
All inputs are finite; a program needn't handle non-finite values. No bound on the sum of `significance` on one device may be relied on, other than what follows from the above.
Results may differ from a plain program's by a relative error of at most 0.0003.
Values sent between devices are 32-bit elements; how exact they have to be, the bound alone decides.
A program may use at most 128 MiB of HBM per device.

v0:
```python
import jax
import jax.numpy as jnp
from jax import lax
from jax.sharding import PartitionSpec as P

NBAS = 3072
SHELL = 16
TILES_DEV = 32


def place_blocks(values, row_shell, col_shell, row_count, col_count):
    slots = values.shape[0]
    row_hot = (row_shell[:, None] == jnp.arange(row_count, dtype=jnp.int32)[None, :]).astype(
        jnp.float32
    )
    col_hot = (col_shell[:, None] == jnp.arange(col_count, dtype=jnp.int32)[None, :]).astype(
        jnp.float32
    )
    spread = row_hot[:, :, None, None] * values.reshape(slots, 1, SHELL, SHELL)
    spread = spread.reshape(slots, row_count * SHELL * SHELL)
    placed = jnp.dot(
        spread.T, col_hot, precision=lax.Precision.HIGHEST, preferred_element_type=jnp.float32
    )
    placed = placed.reshape(row_count, SHELL, SHELL, col_count)
    return jnp.transpose(placed, (0, 1, 3, 2)).reshape(row_count * SHELL, col_count * SHELL)


def shards(eri, owner, quartet, significance, density):
    group_size = lax.axis_size("gx")
    shell_count = NBAS // SHELL
    slab_shells = shell_count // (group_size * lax.axis_size("gz"))
    col_shells = shell_count // lax.axis_size("gy")
    capacity = min(TILES_DEV, 2 * TILES_DEV // group_size)
    pair_size = SHELL * SHELL
    all_slots = group_size * capacity
    density_blocks = density.reshape(density.shape[0] // SHELL, SHELL, shell_count, SHELL)
    target = owner[:, 0]
    onehot = (target[:, None] == jnp.arange(group_size, dtype=jnp.int32)[None, :]).astype(jnp.int32)
    before = jnp.cumsum(onehot, axis=0) - onehot
    place_in = jnp.sum(before * onehot, axis=1)
    position = target * capacity + place_in
    placement = jnp.arange(all_slots, dtype=jnp.int32)[:, None] == position[None, :]
    blocks = density_blocks[quartet[:, 2], :, quartet[:, 3], :]
    flat_block = blocks.reshape(blocks.shape[0], pair_size)
    local_terms = jnp.einsum("tij,tj->ti", eri, flat_block, preferred_element_type=jnp.float32)
    local_terms = local_terms * significance.astype(jnp.float32)[:, None]
    result_buffer = jnp.dot(
        placement.astype(jnp.float32),
        local_terms,
        precision=lax.Precision.HIGHEST,
        preferred_element_type=jnp.float32,
    )
    index_buffer = jnp.sum(placement.astype(jnp.int32)[:, :, None] * quartet[None, :, :2], axis=1)
    summed, indices = (
        lax.all_to_all(result_buffer, "gx", split_axis=0, concat_axis=0, tiled=True),
        lax.all_to_all(index_buffer, "gx", split_axis=0, concat_axis=0, tiled=True),
    )
    every_block, every_index = (
        lax.all_gather(summed, "gy", axis=0, tiled=True),
        lax.all_gather(indices, "gy", axis=0, tiled=True),
    )
    local_ket = (every_index[:, 1] - lax.axis_index("gy") * col_shells).astype(jnp.int32)
    owned_cols = place_blocks(every_block, every_index[:, 0], local_ket, slab_shells, col_shells)
    return lax.all_gather(owned_cols, "gz", axis=0, tiled=True)


def solution(mesh):
    in_specs = (
        P(("gx", "gy", "gz"), None, None),
        P(("gx", "gy", "gz"), None),
        P(("gx", "gy", "gz"), None),
        P(("gx", "gy", "gz")),
        P("gy", None),
    )
    out_specs = P("gx", "gy")
    return jax.shard_map(shards, mesh=mesh, in_specs=in_specs, out_specs=out_specs, check_vma=False)
```

profile of v0, /device:TPU:0, one launch (start us, length us, event | category | flops | bytes accessed | tf_op | source)
XLA Modules:
  0.0 189.2 jit_solution(2160247424836363765)
XLA Ops:
  6.5 0.7 fusion.15
  7.3 0.1 reduce_window_sum.11
  7.3 0.8 select_reduce_fusion
  8.2 0.7 multiply_add_fusion
  8.8 0.7 slice.17
  9.5 0.1 fusion.16
  9.6 0.1 multiply_reduce_fusion
  9.7 0.1 all_to_all.16
  9.8 0.6 copy.28
  10.3 4.3 %all-to-all-start = ((s32[2,32,2]{1,2,0:T(2,128)}), s32[2,32,2]{1,2,0:T(2,128)S(1)}, u32[]{:S(2)}, u32[]{:S(2)}) async-start(s32[2,32,2]{1,2,0:T(2,128)} %copy.28), calls=%async_computation | async-start | bytes 4096 | tf_op jit(solution)/shard_map/all_to_all | solution.py:56
  14.6 0.8 fusion.23
  15.4 34.0 %reshape.74 = bf16[48,16,192,16]{3,2,1,0:T(8,128)(2,1)} reshape(bf16[768,3072]{1,0:T(8,128)(2,1)} %param.9) | data formatting | bytes 9437184 | tf_op jit(solution)/shard_map/reshape | solution.py:36
  49.4 40.7 %copy.31 = bf16[48,16,192,16]{3,1,2,0:T(8,128)(2,1)} copy(bf16[48,16,192,16]{3,2,1,0:T(8,128)(2,1)} %reshape.74) | data formatting | bytes 9437184 | tf_op jit(solution)/shard_map/reshape | solution.py:36
  90.1 1.4 gather_fusion
  91.5 0.2 copy.32
  91.7 0.1 copy.35
  91.8 3.4 %fusion.24 = f32[32,1,256]{2,1,0:T(1,128)S(1)} fusion(bf16[32,256,1]{1,2,0:T(2,128)(2,1)S(1)} %copy.35, bf16[32,256,256]{2,1,0:T(8,128)(2,1)} %param.5), kind=kOutput, calls=%fused_computation.33 | convolution fusion | flops 4194304 | bytes 4243456 | tf_op jit(solution)/shard_map/tij,tj->ti/dot_general | solution.py:45
  95.2 0.9 fusion.10
  96.1 0.0 all-to-all-done
  96.1 3.3 %all-to-all-start.1 = ((f32[2,32,256]{2,1,0:T(8,128)}), f32[2,32,256]{2,1,0:T(8,128)S(1)}, u32[]{:S(2)}, u32[]{:S(2)}) async-start(f32[2,32,256]{2,1,0:T(8,128)} %bitcast.6), calls=%async_computation.1 | async-start | bytes 131072 | tf_op jit(solution)/shard_map/all_to_all | solution.py:55
  99.4 0.0 all-gather.3.cloned.1.call-start
  99.5 0.1 reshape.83
  99.5 11.6 %all-gather = s32[4,64,2]{1,2,0:T(2,128)S(1)} all-gather(s32[1,64,2]{1,2,0:T(2,128)S(1)} %reshape.83), channel_id=1, replica_groups=mesh['gx'=2,'gy'=4,'gz'=4] {'gy'}, dimensions={0}, use_global_device_ids=true | all-gather | bytes 2560 | tf_op jit(solution)/shard_map/all_gather | solution.py:60
  111.2 0.1 reshape.84
  111.3 13.8 %all_gather.10 = f32[256,256]{1,0:T(8,128)S(1)} all-gather(f32[64,256]{1,0:T(8,128)S(1)} %bitcast.42), channel_id=1, replica_groups=mesh['gx'=2,'gy'=4,'gz'=4] {'gy'}, dimensions={0}, use_global_device_ids=true | all-gather | bytes 327680 | tf_op jit(solution)/shard_map/all_gather | solution.py:59
  125.1 0.1 copy.33
  125.3 3.1 %fusion.5 = f32[24,16,48,16]{2,3,1,0:T(8,128)S(1)} fusion(f32[256,16,16]{0,2,1:T(8,128)S(1)} %bitcast.41, f32[256,24]{0,1:T(8,128)S(1)} %fusion.13, s32[256]{0:T(256)S(1)} %bitcast.44), kind=kOutput, calls=%fused_computation.6 | convolution fusion | flops 907554816 | bytes 1467392 | tf_op jit(solution)/shard_map/dot_general | solution.py:21
  128.4 5.1 %copy.34 = f32[24,16,48,16]{3,2,1,0:T(8,128)} copy(f32[24,16,48,16]{2,3,1,0:T(8,128)S(1)} %fusion.5) | data formatting | bytes 2359296 | tf_op jit(solution)/shard_map/transpose | solution.py:25
  133.5 7.6 %reshape.76 = f32[384,768]{1,0:T(8,128)} reshape(f32[24,16,48,16]{3,2,1,0:T(8,128)} %copy.34) | data formatting | bytes 2359296 | tf_op jit(solution)/shard_map/reshape | solution.py:25
  141.2 0.0 all-gather.3.cloned.1.call-update
  141.2 36.3 %all-gather.3.cloned.1.call-done = f32[1536,768]{1,0:T(8,128)} async-done(((f32[384,768]{1,0:T(8,128)}), f32[1536,768]{1,0:T(8,128)}) %all-gather.3.cloned.1.call-update) | async-done | bytes 4718608 | tf_op jit(solution)/shard_map/all_gather | solution.py:64
  177.5 4.8 %copy.43 = f32[1536,768]{1,0:T(8,128)} copy(f32[1536,768]{1,0:T(8,128)} %all-gather.3.cloned.1.call-done) | data formatting | bytes 9437184
  (8 shorter events, 0.0 us)
Async XLA Ops:
  10.3 85.8 %all-to-all-start = ((s32[2,32,2]{1,2,0:T(2,128)}), s32[2,32,2]{1,2,0:T(2,128)S(1)}, u32[]{:S(2)}, u32[]{:S(2)}) async-start(s32[2,32,2]{1,2,0:T(2,128)} %copy.28), calls=%async_computation | async-start | bytes 4096 | tf_op jit(solution)/shard_map/all_to_all | solution.py:56
  49.4 42.4 %copy-start = (s32[32]{0:T(128)S(1)}, s32[32]{0:T(128)}, u32[]{:S(2)}) copy-start(s32[32]{0:T(128)} %param.8) | copy-start | bytes 388
  96.1 15.2 %all-to-all-start.1 = ((f32[2,32,256]{2,1,0:T(8,128)}), f32[2,32,256]{2,1,0:T(8,128)S(1)}, u32[]{:S(2)}, u32[]{:S(2)}) async-start(f32[2,32,256]{2,1,0:T(8,128)} %bitcast.6), calls=%async_computation.1 | async-start | bytes 131072 | tf_op jit(solution)/shard_map/all_to_all | solution.py:55
  99.4 78.1 %all-gather.3.cloned.1.call-start = ((), (), s32[]{:S(2)}) async-start(), calls=%async_computation.2 | async-start | bytes 5898240 | tf_op jit(solution)/shard_map/all_gather | solution.py:64
Sparse Core Ops, SparseCore 0:
  141.3 36.1 all-gather.2
where the time goes:
time: 191 us; the launch traced here: 189 us
  local copies, waits for them, and re-layouts  95.7 us (50%)
  waiting for transfers between devices  36.3 us (19%)
  blocking collectives  25.5 us (13%)
  between operations  13.5 us (7%)
  starting transfers between devices  7.6 us (4%)
  matrix products  7.42 us (4%)
  other arithmetic  3.23 us (2%)
    reshape x2, local copies, waits for them, and re-layouts, shards(): density.reshape(density.shape[0] // SHELL, SHELL, shell_count, SHELL)  74.7 us
    all_gather x1, waiting for transfers between devices, shards(): return lax.all_gather(owned_cols, 'gz', axis=0, tiled=True)  36.3 us
    all_gather x1, blocking collectives, shards(): lax.all_gather(summed, 'gy', axis=0, tiled=True)  13.8 us
    all_gather x1, blocking collectives, shards(): lax.all_gather(indices, 'gy', axis=0, tiled=True)  11.6 us
    reshape x1, local copies, waits for them, and re-layouts, place_blocks(): jnp.transpose(placed, (0, 1, 3, 2))  7.64 us
    transpose x1, local copies, waits for them, and re-layouts, place_blocks(): jnp.transpose(placed, (0, 1, 3, 2))  5.15 us
    unnamed x5, local copies, waits for them, and re-layouts  4.99 us
    all_to_all x1, starting transfers between devices, shards(): lax.all_to_all(index_buffer, 'gx', split_axis=0, concat_axis=0, tiled=True)  4.26 us
  transfers between devices with their start and end apart: 3, of which 1 were waited for; matrix products, arithmetic and copies ran while one was open for 43% of the time, Pallas kernels for 0%

commit v1 on v0

v1 whole, which is shorter than its diff:
```python
import functools

import jax
import jax.numpy as jnp
from jax import lax
from jax.experimental import pallas as pl
from jax.experimental.pallas import tpu as pltpu
from jax.sharding import PartitionSpec as P

SHELL = 16
PACK = 128 // SHELL
MESH = pl.DeviceIdType.MESH


def iota(shape, dim):
    return lax.broadcasted_iota(jnp.int32, shape, dim)


def contract_kernel(ket_bits, row_bits, owner_ref, quartet_ref, keep_ref, eri_ref, density_ref,
                    out_ref, tiles, picked, masked, tile_sem, pick_sem):
    count = eri_ref.shape[0]
    groups = count // PACK
    picks = []
    for t in range(count):
        row = pl.multiple_of(quartet_ref[t, 2] * SHELL, SHELL)
        col = pl.multiple_of((quartet_ref[t, 3] // PACK) * 128, 128)
        pick = pltpu.make_async_copy(density_ref.at[pl.ds(row, SHELL), pl.ds(col, 128)],
                                     picked.at[pl.ds(t * SHELL, SHELL), :], pick_sem.at[t])
        pick.start()
        picks.append(pick)
    loads = []
    for g in range(groups):
        part = pl.ds(g * PACK, PACK)
        load = pltpu.make_async_copy(eri_ref.at[part], tiles.at[part], tile_sem.at[g])
        load.start()
        loads.append(load)

    lane = iota((8, 128), 1)
    codes = jnp.zeros((8, 128), jnp.int32)
    for t in range(count):
        code = (owner_ref[t, 0] << (ket_bits + row_bits)) + (quartet_ref[t, 0] << ket_bits) + quartet_ref[t, 1]
        codes = jnp.where(lane == t, code, codes)
    out_ref[pl.ds(groups * SHELL, 8), :] = codes.astype(jnp.float32)

    block_lane = iota((SHELL, 128), 1) // SHELL
    for t in range(count):
        picks[t].wait()
        place = jnp.where(keep_ref[t] > 0, lax.rem(quartet_ref[t, 3], PACK), -1)
        rows = pl.ds(t * SHELL, SHELL)
        block = picked[rows, :].astype(jnp.float32)
        masked[rows, :] = jnp.where(block_lane == place, block, 0.0).astype(jnp.bfloat16)

    pair = SHELL * SHELL
    repeat = (iota((128, pair), 0) % SHELL == iota((128, pair), 1) % SHELL).astype(jnp.bfloat16)
    own_row = iota((128, pair), 0) % SHELL == iota((128, pair), 1) // SHELL
    same_tile = (iota((128, 128), 0) // SHELL == iota((128, 128), 1) // SHELL).astype(jnp.bfloat16)
    weights = []
    for g in range(groups):
        spread = jnp.dot(masked[pl.ds(g * 128, 128), :], repeat, preferred_element_type=jnp.float32)
        spread = jnp.where(own_row, spread, 0.0).astype(jnp.bfloat16)
        flat = jnp.dot(same_tile, spread, preferred_element_type=jnp.float32)
        weights.append(flat.T.astype(jnp.bfloat16))

    tile_of_lane = iota((pair, 128), 1) // SHELL
    diagonal = iota((pair, 128), 0) % SHELL == iota((pair, 128), 1) % SHELL
    for g in range(groups):
        loads[g].wait()
        total = jnp.zeros((pair, 128), jnp.float32)
        for i in range(PACK):
            result = jnp.dot(tiles[g * PACK + i], weights[g], preferred_element_type=jnp.float32)
            total = jnp.where(tile_of_lane == i, result, total)
        total = jnp.where(diagonal, total, 0.0).reshape(SHELL, SHELL, 128)
        out_ref[pl.ds(g * SHELL, SHELL), :] = jnp.sum(total, axis=1)


def gather_kernel(colors, sizes, own_ref, all_ref, send_sem, recv_sem, local_sem):
    gx, gy, gz = lax.axis_index("gx"), lax.axis_index("gy"), lax.axis_index("gz")
    mine = {"c": lax.rem(gz, 2), "x": lax.div(gz, 2), "y": gx, "z": gy}
    dims = ("c", "x", "y", "z")

    def device(where):
        return {"gx": where["y"], "gy": where["z"], "gz": where["x"] * 2 + where["c"]}

    def peer(dim, step):
        return device(dict(mine, **{dim: lax.rem(mine[dim] + step, sizes[dim])}))

    barrier = pltpu.get_barrier_semaphore()
    greeted = 0
    for dim in dims:
        for step in range(1, sizes[dim]):
            pl.semaphore_signal(barrier, inc=1, device_id=peer(dim, step), device_id_type=MESH)
            greeted += 1
    pl.semaphore_wait(barrier, greeted)

    here = pltpu.make_async_copy(
        own_ref, all_ref.at[mine["c"], mine["x"], mine["y"], mine["z"]], local_sem)
    here.start()

    pending = [[] for _ in colors]
    slot = 0
    for stage in range(len(dims)):
        for number, (first, rows, order) in enumerate(colors):
            for copy in pending[number]:
                copy.wait()
            pending[number] = []
            if stage == 1 and number == 0:
                here.wait()
            dim, done = order[stage], order[:stage]
            part = pl.ds(first, rows)
            index = tuple(pl.ds(0, sizes[d]) if d in done else mine[d] for d in dims)
            held = all_ref.at[index + (part,)]
            for step in range(1, sizes[dim]):
                copy = pltpu.make_async_remote_copy(
                    src_ref=own_ref.at[part] if stage == 0 else held, dst_ref=held,
                    send_sem=send_sem.at[slot], recv_sem=recv_sem.at[slot],
                    device_id=peer(dim, step), device_id_type=MESH)
                copy.start()
                pending[number].append(copy)
                slot += 1
    for copies in pending:
        for copy in copies:
            copy.wait()


def scatter_kernel(ket_bits, row_bits, row_shells, col_shells, width, all_ref, out_ref,
                   orders, order_smem, order_sem, out_sem, *slabs):
    cores, xs, ys, zs = all_ref.shape[:4]
    groups = all_ref.shape[4] // SHELL
    slab_rows = row_shells * SHELL
    code = all_ref[:, :, :, :, groups * SHELL, :].reshape(cores * xs * ys * zs, 128).astype(jnp.int32)
    ket = (code & ((1 << ket_bits) - 1)) - lax.axis_index("gy") * col_shells
    row = (code >> ket_bits) & ((1 << row_bits) - 1)
    owner = code >> (ket_bits + row_bits)
    valid = (owner == lax.axis_index("gx")) & (ket >= 0) & (ket < col_shells)
    orders[...] = jnp.where(valid, (row << ket_bits) + ket, row_shells << ket_bits)
    fetch = pltpu.make_async_copy(orders, order_smem, order_sem)
    fetch.start()

    def clear(shell, carry):
        for slab in slabs:
            slab[pl.ds(pl.multiple_of(shell * SHELL, SHELL), SHELL), :] = jnp.zeros((SHELL, width), jnp.float32)
        return carry

    lax.fori_loop(0, row_shells, clear, 0)
    fetch.wait()
    block_lane = iota((SHELL, 128), 1) // SHELL

    def add(step, carry):
        source, group = step // groups, step % groups
        y, z = source // zs, source % zs
        first = pl.multiple_of(group * SHELL, SHELL)
        values = [all_ref[s % 2, s // 2, y, z, pl.ds(first, SHELL), :] for s in range(len(slabs))]
        for i in range(PACK):
            for s, slab in enumerate(slabs):
                line = ((s % 2) * xs + s // 2) * ys * zs + source
                order = order_smem[line, group * PACK + i]
                shell = order >> ket_bits
                local = order & ((1 << ket_bits) - 1)
                spot = local & (PACK - 1)
                moved = pltpu.roll(values[s], ((spot - i) * SHELL) & 127, 1)
                moved = jnp.where(block_lane == spot, moved, 0.0)
                rows = pl.ds(pl.multiple_of(shell * SHELL, SHELL), SHELL)
                cols = pl.ds(pl.multiple_of((local // PACK) * 128, 128), 128)
                slab[rows, cols] = slab[rows, cols] + moved
        return carry

    lax.fori_loop(0, ys * zs * groups, add, 0)
    stores = []
    for s, slab in enumerate(slabs):
        store = pltpu.make_async_copy(slab.at[pl.ds(0, slab_rows), :],
                                      out_ref.at[pl.ds(s * slab_rows, slab_rows), :], out_sem.at[s])
        store.start()
        stores.append(store)
    for store in stores:
        store.wait()


def color_rows(rows):
    units = rows // 8
    first = max(1, units // 9)
    second = max(1, (units - first) * 3 // 8)
    third = units - first - second
    return [(0, first * 8, "xyzc"), (first * 8, second * 8, "yzxc"), ((first + second) * 8, third * 8, "zxyc")]


def solution(mesh):
    n_gx, n_gy, n_gz = mesh.shape["gx"], mesh.shape["gy"], mesh.shape["gz"]

    def shards(eri, owner, quartet, significance, density):
        tiles, pair = eri.shape[0], eri.shape[1]
        shells = density.shape[1] // SHELL
        row_shells, col_shells = shells // (n_gx * n_gz), shells // n_gy
        ket_bits, row_bits = (shells - 1).bit_length(), (row_shells - 1).bit_length()
        rows = tiles // PACK * SHELL + 8
        smem, hbm = pl.BlockSpec(memory_space=pltpu.SMEM), pl.BlockSpec(memory_space=pl.ANY)
        vmem = pl.BlockSpec(memory_space=pltpu.VMEM)
        limit = 48 * 1024 * 1024
        own = pl.pallas_call(
            functools.partial(contract_kernel, ket_bits, row_bits),
            out_shape=jax.ShapeDtypeStruct((rows, 128), jnp.float32),
            in_specs=[smem, smem, smem, hbm, hbm],
            out_specs=vmem,
            scratch_shapes=[
                pltpu.VMEM(eri.shape, jnp.bfloat16),
                pltpu.VMEM((tiles * SHELL, 128), jnp.bfloat16),
                pltpu.VMEM((tiles * SHELL, 128), jnp.bfloat16),
                pltpu.SemaphoreType.DMA((tiles // PACK,)),
                pltpu.SemaphoreType.DMA((tiles,)),
            ],
            compiler_params=pltpu.CompilerParams(vmem_limit_bytes=limit),
            name="contract",
        )(owner, quartet, significance, eri, density)

        sizes = {"c": 2, "x": n_gz // 2, "y": n_gx, "z": n_gy}
        colors = color_rows(rows)
        slots = len(colors) * sum(size - 1 for size in sizes.values())
        everyone = pl.pallas_call(
            functools.partial(gather_kernel, colors, sizes),
            out_shape=jax.ShapeDtypeStruct((2, n_gz // 2, n_gx, n_gy, rows, 128), jnp.float32),
            in_specs=[vmem],
            out_specs=vmem,
            scratch_shapes=[
                pltpu.SemaphoreType.DMA((slots,)),
                pltpu.SemaphoreType.DMA((slots,)),
                pltpu.SemaphoreType.DMA,
            ],
            compiler_params=pltpu.CompilerParams(
                collective_id=0, has_side_effects=True, vmem_limit_bytes=limit),
            name="gather",
        )(own)

        width = -(-col_shells * SHELL // 128) * 128
        devices = n_gx * n_gy * n_gz
        out = pl.pallas_call(
            functools.partial(scatter_kernel, ket_bits, row_bits, row_shells, col_shells, width),
            out_shape=jax.ShapeDtypeStruct((n_gz * row_shells * SHELL, width), jnp.float32),
            in_specs=[vmem],
            out_specs=hbm,
            scratch_shapes=[
                pltpu.VMEM((devices, 128), jnp.int32),
                pltpu.SMEM((devices, 128), jnp.int32),
                pltpu.SemaphoreType.DMA,
                pltpu.SemaphoreType.DMA((n_gz,)),
            ] + [pltpu.VMEM(((row_shells + 1) * SHELL, width), jnp.float32)] * n_gz,
            compiler_params=pltpu.CompilerParams(vmem_limit_bytes=limit),
            name="scatter",
        )(everyone)
        return out if width == col_shells * SHELL else out[:, :col_shells * SHELL]

    in_specs = (
        P(("gx", "gy", "gz"), None, None),
        P(("gx", "gy", "gz"), None),
        P(("gx", "gy", "gz"), None),
        P(("gx", "gy", "gz")),
        P("gy", None),
    )
    return jax.shard_map(shards, mesh=mesh, in_specs=in_specs, out_specs=P("gx", "gy"), check_vma=False)
```

time: 191 us -> 40.9 us (0.21)
  local copies, waits for them, and re-layouts: 95.7 us -> 4.34 us
  Pallas kernels: 0 us -> 36.3 us
  waiting for transfers between devices: 36.3 us -> 0 us
  blocking collectives: 25.5 us -> 0 us
  between operations: 13.5 us -> 0.02 us
  starting transfers between devices: 7.6 us -> 0 us
  matrix products: 7.42 us -> 0 us
  other arithmetic: 3.23 us -> 0 us
    reshape x4 -> x0, local copies, waits for them, and re-layouts: 82.5 us -> none  [the longest x2 74.7 us: shards(): density.reshape(density.shape[0] // SHELL, SHELL, shell_count, SHELL)]
    pallas_call x0 -> x3, Pallas kernels: none -> 36.3 us  [the longest x1 19.2 us: shards(): pl.pallas_call(functools.partial(gather_kernel, colors, sizes), out_shape...]
    all_gather x1 -> x0, waiting for transfers between devices: 36.3 us -> none  [shards(): return lax.all_gather(owned_cols, 'gz', axis=0, tiled=True)]
    all_gather x2 -> x0, blocking collectives: 25.5 us -> none  [the longest x1 13.8 us: shards(): lax.all_gather(summed, 'gy', axis=0, tiled=True)]
    all_to_all x2 -> x0, starting transfers between devices: 7.56 us -> none  [the longest x1 4.26 us: shards(): lax.all_to_all(index_buffer, 'gx', split_axis=0, concat_axis=0, tiled=True)]
    dot_general x3 -> x0, matrix products: 7.42 us -> none  [the longest x1 3.36 us: shards(): jnp.einsum('tij,tj->ti', eri, flat_block, preferred_element_type=jnp.floa...]
    transpose x1 -> x0, local copies, waits for them, and re-layouts: 5.15 us -> none  [place_blocks(): jnp.transpose(placed, (0, 1, 3, 2))]
    unnamed x5 -> x6, local copies, waits for them, and re-layouts: 4.99 us -> 4.34 us
  transfers between devices with their start and end apart: 3 -> 0, of which waited for: 1 -> 0; matrix products, arithmetic and copies ran while one was open for 43% -> 0% of each run, Pallas kernels for 0% -> 0%
where the time goes in v1:
time: 40.9 us; the launch traced here: 40.7 us
  Pallas kernels  36.3 us (89%)
  local copies, waits for them, and re-layouts  4.34 us (11%)
    pallas_call x1, Pallas kernels, shards(): pl.pallas_call(functools.partial(gather_kernel, colors, sizes), out_shape...  19.2 us
    pallas_call x1, Pallas kernels, shards(): pl.pallas_call(functools.partial(scatter_kernel, ket_bits, row_bits, row_...  12.4 us
    pallas_call x1, Pallas kernels, shards(): pl.pallas_call(functools.partial(contract_kernel, ket_bits, row_bits), ou...  4.68 us
    unnamed x6, local copies, waits for them, and re-layouts  4.34 us

profile of v1, /device:TPU:0, one launch (start us, length us, event | category | flops | bytes accessed | tf_op | source)
XLA Modules:
  0.0 40.7 jit_solution(12794234382321452249)
XLA Ops:
  0.0 0.7 %copy.6.owner_ref = s32[32,1]{1,0:T(8,128)S(1)} copy(s32[32,1]{0,1:T(1,128)} %param.6) | data formatting | bytes 256 | tf_op args[1]
  0.7 0.8 %copy.7.quartet_ref = s32[32,4]{1,0:T(8,128)S(1)} copy(s32[32,4]{0,1:T(4,128)} %param.7) | data formatting | bytes 1024 | tf_op args[2]
  1.5 0.0 copy-start
  1.5 2.2 %copy-done = bf16[32,256,256]{2,1,0:T(8,128)(2,1)S(1)} copy-done((bf16[32,256,256]{2,1,0:T(8,128)(2,1)S(1)}, bf16[32,256,256]{2,1,0:T(8,128)(2,1)}, u32[]{:S(2)}) %copy-start) | copy-done | bytes 4194328
  3.7 0.0 copy-start.1
  3.7 0.7 %copy-done.1 = s32[32]{0:T(128)S(1)} copy-done((s32[32]{0:T(128)S(1)}, s32[32]{0:T(128)}, u32[]{:S(2)}) %copy-start.1) | copy-done | bytes 152
  4.3 4.7 %contract.1.own_ref = f32[72,128]{1,0:T(8,128)S(1)} custom-call(s32[32,1]{1,0:T(8,128)S(1)} %copy.6.owner_ref, s32[32,4]{1,0:T(8,128)S(1)} %copy.7.quartet_ref, s32[32]{0:T(128)S(1)} %copy-done.1, bf16[32,256,256]{2,1,0:T(8,128)(2,1)S(1)} %copy-done, bf16[768,3072]{1,0:T(8,128)(2,1)} %density_ref.1), custom_call_target="tpu_custom_call" | custom-call | tf_op jit(solution)/shard_map/contract/pallas_call | solution.py:198
  9.0 19.2 %gather.1.all_ref = f32[2,2,2,4,72,128]{5,4,3,2,1,0:T(8,128)S(1)} custom-call(f32[72,128]{1,0:T(8,128)S(1)} %contract.1.own_ref), custom_call_target="tpu_custom_call" | custom-call | tf_op jit(solution)/shard_map/gather/pallas_call | solution.py:217
  28.3 12.4 %scatter.1 = f32[1536,768]{1,0:T(8,128)} custom-call(f32[2,2,2,4,72,128]{5,4,3,2,1,0:T(8,128)S(1)} %gather.1.all_ref), custom_call_target="tpu_custom_call" | custom-call | tf_op jit(solution)/shard_map/scatter/pallas_call | solution.py:234
Async XLA Ops:
  1.5 2.2 %copy-start = (bf16[32,256,256]{2,1,0:T(8,128)(2,1)S(1)}, bf16[32,256,256]{2,1,0:T(8,128)(2,1)}, u32[]{:S(2)}) copy-start(bf16[32,256,256]{2,1,0:T(8,128)(2,1)} %eri_ref.1) | copy-start | bytes 12582916
  3.7 0.7 %copy-start.1 = (s32[32]{0:T(128)S(1)}, s32[32]{0:T(128)}, u32[]{:S(2)}) copy-start(s32[32]{0:T(128)} %keep_ref.1) | copy-start | bytes 388

commit v2 on v1

v2 whole, which is shorter than its diff:
```python
import functools

import jax
import jax.numpy as jnp
from jax import lax
from jax.experimental import pallas as pl
from jax.experimental.pallas import tpu as pltpu
from jax.sharding import PartitionSpec as P

SHELL = 16
PACK = 128 // SHELL
MESH = pl.DeviceIdType.MESH


def iota(shape, dim):
    return lax.broadcasted_iota(jnp.int32, shape, dim)


def contract_kernel(ket_bits, row_bits, owner_ref, quartet_ref, keep_ref, eri_ref, density_ref,
                    out_ref, tiles, picked, masked, tile_sem, pick_sem):
    count = eri_ref.shape[0]
    groups = count // PACK
    picks = []
    for t in range(count):
        row = pl.multiple_of(quartet_ref[2, t] * SHELL, SHELL)
        col = pl.multiple_of((quartet_ref[3, t] // PACK) * 128, 128)
        pick = pltpu.make_async_copy(density_ref.at[pl.ds(row, SHELL), pl.ds(col, 128)],
                                     picked.at[pl.ds(t * SHELL, SHELL), :], pick_sem.at[t])
        pick.start()
        picks.append(pick)
    loads = []
    for g in range(groups):
        part = pl.ds(g * PACK, PACK)
        load = pltpu.make_async_copy(eri_ref.at[part], tiles.at[part], tile_sem.at[g])
        load.start()
        loads.append(load)

    lane = iota((8, 128), 1)
    codes = jnp.zeros((8, 128), jnp.int32)
    for t in range(count):
        code = (owner_ref[0, t] << (ket_bits + row_bits)) + (quartet_ref[0, t] << ket_bits) + quartet_ref[1, t]
        codes = jnp.where(lane == t, code, codes)
    out_ref[pl.ds(groups * SHELL, 8), :] = codes.astype(jnp.float32)

    block_lane = iota((SHELL, 128), 1) // SHELL
    for t in range(count):
        picks[t].wait()
        place = jnp.where(keep_ref[t] > 0, lax.rem(quartet_ref[3, t], PACK), -1)
        rows = pl.ds(t * SHELL, SHELL)
        block = picked[rows, :].astype(jnp.float32)
        masked[rows, :] = jnp.where(block_lane == place, block, 0.0).astype(jnp.bfloat16)

    pair = SHELL * SHELL
    repeat = (iota((128, pair), 0) % SHELL == iota((128, pair), 1) % SHELL).astype(jnp.bfloat16)
    own_row = iota((128, pair), 0) % SHELL == iota((128, pair), 1) // SHELL
    same_tile = (iota((128, 128), 0) // SHELL == iota((128, 128), 1) // SHELL).astype(jnp.bfloat16)
    weights = []
    for g in range(groups):
        spread = jnp.dot(masked[pl.ds(g * 128, 128), :], repeat, preferred_element_type=jnp.float32)
        spread = jnp.where(own_row, spread, 0.0).astype(jnp.bfloat16)
        flat = jnp.dot(same_tile, spread, preferred_element_type=jnp.float32)
        weights.append(flat.T.astype(jnp.bfloat16))

    tile_of_lane = iota((pair, 128), 1) // SHELL
    diagonal = iota((pair, 128), 0) % SHELL == iota((pair, 128), 1) % SHELL
    for g in range(groups):
        loads[g].wait()
        total = jnp.zeros((pair, 128), jnp.float32)
        for i in range(PACK):
            result = jnp.dot(tiles[g * PACK + i], weights[g], preferred_element_type=jnp.float32)
            total = jnp.where(tile_of_lane == i, result, total)
        total = jnp.where(diagonal, total, 0.0).reshape(SHELL, SHELL, 128)
        out_ref[pl.ds(g * SHELL, SHELL), :] = jnp.sum(total, axis=1)


def other(index, step, size):
    if size & (size - 1):
        return lax.rem(index + step, size)
    bit = 1
    while bit <= step:
        if step & bit:
            index = index + bit - 2 * bit * lax.rem(lax.div(index, bit), 2)
        bit *= 2
    return index


def source_of(index, step, size):
    return lax.rem(index + size - step, size) if size & (size - 1) else other(index, step, size)


def gather_kernel(sizes, own_ref, all_ref, send_sem, recv_sem, local_sem):
    gx, gy, gz = lax.axis_index("gx"), lax.axis_index("gy"), lax.axis_index("gz")
    core, x, y, z = lax.rem(gz, 2), lax.div(gz, 2), gx, gy
    xs, ys, zs = sizes

    def device(core, x, y, z):
        return {"gx": y, "gy": z, "gz": x * 2 + core}

    plane = [(dx, dy) for dx in range(xs) for dy in range(ys) if dx or dy]
    plane.sort(key=lambda step: (-(step[0] > 0) - (step[1] > 0), step))
    flat = {step: device(core, other(x, step[0], xs), other(y, step[1], ys), z) for step in plane}
    column = {step: device(core, x, y, other(z, step, zs)) for step in range(1, zs)}
    twin = device(1 - core, x, y, z)

    barrier = pltpu.get_barrier_semaphore()
    peers = list(flat.values()) + list(column.values()) + [twin]
    for peer in peers:
        pl.semaphore_signal(barrier, inc=1, device_id=peer, device_id_type=MESH)
    pl.semaphore_wait(barrier, len(peers))

    slots = iter(range(send_sem.shape[0]))

    def send(source, place, peer):
        slot = next(slots)
        copy = pltpu.make_async_remote_copy(
            src_ref=source, dst_ref=all_ref.at[place], send_sem=send_sem.at[slot],
            recv_sem=recv_sem.at[slot], device_id=peer, device_id_type=MESH)
        copy.start()
        return copy

    here = pltpu.make_async_copy(own_ref, all_ref.at[core, x, y, z], local_sem)
    here.start()
    sent, arrivals = [], []

    def spread(source, place):
        for step in plane:
            arrivals.append((send(source, place, flat[step]), step, place[3]))
        sent.append(send(source, place, twin))

    place = (core, x, y, z)
    steps = [send(own_ref, place, column[step]) for step in range(1, zs)]
    spread(own_ref, place)
    for step, copy in enumerate(steps, 1):
        copy.wait_recv()
        place = (core, x, y, source_of(z, step, zs))
        spread(all_ref.at[place], place)
    for copy, (dx, dy), depth in arrivals:
        copy.wait_recv()
        place = (core, source_of(x, dx, xs), source_of(y, dy, ys), depth)
        sent.append(send(all_ref.at[place], place, twin))
    for copy in sent:
        copy.wait_recv()
    for copy in steps + [copy for copy, _, _ in arrivals] + sent:
        copy.wait_send()
    here.wait()


def scatter_kernel(ket_bits, row_bits, row_shells, col_shells, width, all_ref, out_ref,
                   table, table_smem, table_sem, out_sem, *slabs):
    cores, xs, ys, zs = all_ref.shape[:4]
    groups = all_ref.shape[4] // SHELL
    lines = cores * xs * ys * zs
    slab_rows = row_shells * SHELL
    tall = slab_rows + SHELL
    code = all_ref[:, :, :, :, groups * SHELL, :].reshape(lines, 128).astype(jnp.int32)
    ket = (code & ((1 << ket_bits) - 1)) - lax.axis_index("gy") * col_shells
    row = (code >> ket_bits) & ((1 << row_bits) - 1)
    owner = code >> (ket_bits + row_bits)
    valid = (owner == lax.axis_index("gx")) & (ket >= 0) & (ket < col_shells)
    spot = (ket // PACK) * tall + row * SHELL
    table[pl.ds(0, lines), :] = jnp.where(valid, spot, slab_rows)
    table[pl.ds(lines, lines), :] = ((ket - iota((lines, 128), 1)) * SHELL) & 127
    fetch = pltpu.make_async_copy(table, table_smem, table_sem)
    fetch.start()

    def clear(shell, carry):
        rows = pl.ds(pl.multiple_of(shell * 2 * SHELL, SHELL), 2 * SHELL)
        for slab in slabs:
            slab[rows, :] = jnp.zeros((2 * SHELL, 128), jnp.float32)
        return carry

    lax.fori_loop(0, slabs[0].shape[0] // (2 * SHELL), clear, 0)
    fetch.wait()
    block_lane = iota((SHELL, 128), 1) // SHELL

    def add(step, carry):
        source, group = step // groups, step % groups
        y, z = source // zs, source % zs
        first = pl.multiple_of(group * SHELL, SHELL)
        values = [all_ref[s % 2, s // 2, y, z, pl.ds(first, SHELL), :] for s in range(len(slabs))]
        for i in range(PACK):
            for s, slab in enumerate(slabs):
                line = ((s % 2) * xs + s // 2) * ys * zs + source
                lane = group * PACK + i
                moved = pltpu.roll(jnp.where(block_lane == i, values[s], 0.0), table_smem[lines + line, lane], 1)
                rows = pl.ds(pl.multiple_of(table_smem[line, lane], SHELL), SHELL)
                slab[rows, :] = slab[rows, :] + moved
        return carry

    lax.fori_loop(0, ys * zs * groups, add, 0)
    stores = []
    for s, slab in enumerate(slabs):
        for block in range(width // 128):
            store = pltpu.make_async_copy(
                slab.at[pl.ds(block * tall, slab_rows), :],
                out_ref.at[pl.ds(s * slab_rows, slab_rows), pl.ds(block * 128, 128)],
                out_sem.at[s, block])
            store.start()
            stores.append(store)
    for store in stores:
        store.wait()


def solution(mesh):
    n_gx, n_gy, n_gz = mesh.shape["gx"], mesh.shape["gy"], mesh.shape["gz"]

    def shards(eri, owner, quartet, significance, density):
        tiles, pair = eri.shape[0], eri.shape[1]
        shells = density.shape[1] // SHELL
        row_shells, col_shells = shells // (n_gx * n_gz), shells // n_gy
        ket_bits, row_bits = (shells - 1).bit_length(), (row_shells - 1).bit_length()
        rows = tiles // PACK * SHELL + 8
        smem, hbm = pl.BlockSpec(memory_space=pltpu.SMEM), pl.BlockSpec(memory_space=pl.ANY)
        vmem = pl.BlockSpec(memory_space=pltpu.VMEM)
        limit = 48 * 1024 * 1024
        own = pl.pallas_call(
            functools.partial(contract_kernel, ket_bits, row_bits),
            out_shape=jax.ShapeDtypeStruct((rows, 128), jnp.float32),
            in_specs=[smem, smem, smem, pl.BlockSpec(memory_space=pltpu.HBM), hbm],
            out_specs=vmem,
            scratch_shapes=[
                pltpu.VMEM(eri.shape, jnp.bfloat16),
                pltpu.VMEM((tiles * SHELL, 128), jnp.bfloat16),
                pltpu.VMEM((tiles * SHELL, 128), jnp.bfloat16),
                pltpu.SemaphoreType.DMA((tiles // PACK,)),
                pltpu.SemaphoreType.DMA((tiles,)),
            ],
            compiler_params=pltpu.CompilerParams(vmem_limit_bytes=60 * 1024 * 1024),
            name="contract",
        )(owner.T, quartet.T, significance, eri, density)

        sizes = (n_gz // 2, n_gx, n_gy)
        plane = sizes[0] * sizes[1]
        slots = n_gy - 1 + n_gy * (plane - 1) + n_gy * plane
        everyone = pl.pallas_call(
            functools.partial(gather_kernel, sizes),
            out_shape=jax.ShapeDtypeStruct((2, n_gz // 2, n_gx, n_gy, rows, 128), jnp.float32),
            in_specs=[vmem],
            out_specs=vmem,
            scratch_shapes=[
                pltpu.SemaphoreType.DMA((slots,)),
                pltpu.SemaphoreType.DMA((slots,)),
                pltpu.SemaphoreType.DMA,
            ],
            compiler_params=pltpu.CompilerParams(
                collective_id=0, has_side_effects=True, vmem_limit_bytes=limit),
            name="gather",
        )(own)

        width = -(-col_shells * SHELL // 128) * 128
        devices = n_gx * n_gy * n_gz
        out = pl.pallas_call(
            functools.partial(scatter_kernel, ket_bits, row_bits, row_shells, col_shells, width),
            out_shape=jax.ShapeDtypeStruct((n_gz * row_shells * SHELL, width), jnp.float32),
            in_specs=[vmem],
            out_specs=hbm,
            scratch_shapes=[
                pltpu.VMEM((2 * devices, 128), jnp.int32),
                pltpu.SMEM((2 * devices, 128), jnp.int32),
                pltpu.SemaphoreType.DMA,
                pltpu.SemaphoreType.DMA((n_gz, width // 128)),
            ] + [pltpu.VMEM((-(-(row_shells + 1) * (width // 128) // 2) * 2 * SHELL, 128), jnp.float32)] * n_gz,
            compiler_params=pltpu.CompilerParams(vmem_limit_bytes=limit),
            name="scatter",
        )(everyone)
        return out if width == col_shells * SHELL else out[:, :col_shells * SHELL]

    in_specs = (
        P(("gx", "gy", "gz"), None, None),
        P(("gx", "gy", "gz"), None),
        P(("gx", "gy", "gz"), None),
        P(("gx", "gy", "gz")),
        P("gy", None),
    )
    return jax.shard_map(shards, mesh=mesh, in_specs=in_specs, out_specs=P("gx", "gy"), check_vma=False)
```

time: 40.9 us -> 32 us (0.78)
  Pallas kernels: 36.3 us -> 31 us
  local copies, waits for them, and re-layouts: 4.34 us -> 0.76 us
    unnamed x6 -> x2, local copies, waits for them, and re-layouts: 4.34 us -> 0.76 us
    pallas_call x1, Pallas kernels: 12.4 us -> 8.94 us  [shards(): pl.pallas_call(functools.partial(scatter_kernel, ket_bits, row_bits, row_...]
    pallas_call x1, Pallas kernels: 19.2 us -> 15.9 us  [shards(): pl.pallas_call(functools.partial(gather_kernel, sizes), out_shape=jax.Sha...]
    pallas_call x1, Pallas kernels: 4.68 us -> 6.11 us  [shards(): pl.pallas_call(functools.partial(contract_kernel, ket_bits, row_bits), ou...]
where the time goes in v2:
time: 32 us; the launch traced here: 31.7 us
  Pallas kernels  31 us (97%)
  local copies, waits for them, and re-layouts  0.76 us (2%)
    pallas_call x1, Pallas kernels, shards(): pl.pallas_call(functools.partial(gather_kernel, sizes), out_shape=jax.Sha...  15.9 us
    pallas_call x1, Pallas kernels, shards(): pl.pallas_call(functools.partial(scatter_kernel, ket_bits, row_bits, row_...  8.94 us
    pallas_call x1, Pallas kernels, shards(): pl.pallas_call(functools.partial(contract_kernel, ket_bits, row_bits), ou...  6.11 us
    unnamed x2, local copies, waits for them, and re-layouts  0.76 us

profile of v2, /device:TPU:0, one launch (start us, length us, event | category | flops | bytes accessed | tf_op | source)
XLA Modules:
  0.0 31.7 jit_solution(11318272067447505614)
XLA Ops:
  0.0 6.1 %contract.1.own_ref = f32[72,128]{1,0:T(8,128)} custom-call(s32[1,32]{1,0:T(1,128)} %bitcast.3, s32[4,32]{1,0:T(4,128)} %bitcast.2, s32[32]{0:T(128)} %keep_ref.1, bf16[32,256,256]{2,1,0:T(8,128)(2,1)} %eri_ref.1, bf16[768,3072]{1,0:T(8,128)(2,1)} %density_ref.1), custom_call_target="tpu_custom_call" | custom-call | tf_op jit(solution)/shard_map/contract/pallas_call | solution.py:216
  6.1 0.0 copy-start
  6.1 0.8 %copy-done = f32[72,128]{1,0:T(8,128)S(1)} copy-done((f32[72,128]{1,0:T(8,128)S(1)}, f32[72,128]{1,0:T(8,128)}, u32[]{:S(2)}) %copy-start) | copy-done | bytes 36888
  6.9 15.9 %gather.1.all_ref = f32[2,2,2,4,72,128]{5,4,3,2,1,0:T(8,128)S(1)} custom-call(f32[72,128]{1,0:T(8,128)S(1)} %copy-done), custom_call_target="tpu_custom_call" | custom-call | tf_op jit(solution)/shard_map/gather/pallas_call | solution.py:235
  22.8 8.9 %scatter.1 = f32[1536,768]{1,0:T(8,128)} custom-call(f32[2,2,2,4,72,128]{5,4,3,2,1,0:T(8,128)S(1)} %gather.1.all_ref), custom_call_target="tpu_custom_call" | custom-call | tf_op jit(solution)/shard_map/scatter/pallas_call | solution.py:252
Async XLA Ops:
  6.1 0.8 %copy-start = (f32[72,128]{1,0:T(8,128)S(1)}, f32[72,128]{1,0:T(8,128)}, u32[]{:S(2)}) copy-start(f32[72,128]{1,0:T(8,128)} %contract.1.own_ref) | copy-start | bytes 110596
